TPU v7x, 32 devices: a whole 2x2x4 slice. The times are simulated.
32 devices in a mesh: gx: 16 (over z, x, core), gy: 2 (over y).
Axes of the slice: x: 2, y: 2, z: 4, core: 2. Of those that a mesh axis runs over, the one named last changes fastest.
Arguments:
- velocity: float32 [256, 256, 512], P('gx', 'gy'), may hold values from -24 to 24
- viscosity: float32 [256], P('gx'), may hold values from 1000 to 8000
- marker_forces: bfloat16 [4096, 16], P(('gx', 'gy')), may hold values from -18 to 18
- spread_weights: bfloat16 [4096, 16, 2048], P(('gx', 'gy')), may hold values from -1.5 to 1.5
- block_owner: int32 [4096, 1], P(('gx', 'gy')), may hold values from 0 to 31; in each aligned block of 128 rows (0 to 127, 128 to 255, ...) at most 8 rows name the same one
- tile_slot: int32 [4096], P(('gx', 'gy')), may hold values from 0 to 511
Outputs:
- relaxed: float32 [256, 256, 512], P('gx', 'gy')
Inputs may be any that keep to these rules, and one draw needn't show every extreme that they name: `block_owner`: among the 128 blocks held by one device, no owner is named by more than 8 of them.
All inputs are finite; a program needn't handle non-finite values.
Results may differ from a plain program's by a relative error of at most 0.0013.
Values may be sent and summed in bfloat16 or wider, within the bound.
A program may use at most 128 MiB of HBM per device.

v0:
```python
import jax
import jax.numpy as jnp
from jax import lax
from jax.sharding import PartitionSpec as P


def passed_along(x, axis, by):
    length = lax.axis_size(axis)
    pairs = [(i, i + by) for i in range(length) if 0 <= i + by < length]
    return lax.ppermute(x, axis, pairs)


def thomas(below_diag, main_diag, above_diag, right_side):
    count_rows = right_side.shape[0]
    pivot_value = main_diag[0]
    ratios = [above_diag[0] / pivot_value]
    values = [right_side[0] / pivot_value]
    for row_index in range(1, count_rows):
        pivot_value = main_diag[row_index] - below_diag[row_index] * ratios[-1]
        ratios.append(above_diag[row_index] / pivot_value)
        values.append((right_side[row_index] - below_diag[row_index] * values[-1]) / pivot_value)
    result = [values[-1]]
    for row_index in range(count_rows - 2, -1, -1):
        result.append(values[row_index] - ratios[row_index] * result[-1])
    return jnp.stack(result[::-1])


def per_device(velocity, viscosity, marker_forces, spread_weights, block_owner, tile_slot):
    cells_x, cells_y, cells_z = velocity.shape
    line_count = cells_y * cells_z
    grid_x = lax.axis_size("gx")
    grid_y = lax.axis_size("gy")
    devices = grid_x * grid_y
    tile_values = jnp.einsum(
        "bm,bmt->bt", marker_forces, spread_weights, preferred_element_type=jnp.float32
    ).astype(jnp.bfloat16)
    block_count = tile_values.shape[0]
    capacity = max(2, 2 * block_count // devices)
    segment = tile_values.shape[1] // cells_x
    owner_dev = block_owner[:, 0]
    matches = (owner_dev[:, None] == jnp.arange(devices, dtype=jnp.int32)[None, :]).astype(
        jnp.int32
    )
    ranking = jnp.sum(jnp.cumsum(matches, axis=0) * matches, axis=1) - 1
    target = owner_dev * capacity + ranking
    select = target[None, :] == jnp.arange(devices * capacity, dtype=jnp.int32)[:, None]
    outgoing = jnp.dot(
        select.astype(jnp.bfloat16), tile_values, preferred_element_type=jnp.float32
    ).astype(jnp.bfloat16)
    out_slots = (
        jnp.sum(jnp.where(select, tile_slot[None, :], 0), axis=1)
        + jnp.sum(select.astype(jnp.int32), axis=1)
        - 1
    )
    arrived, arrived_slots = (
        lax.all_to_all(
            outgoing.reshape(devices, capacity, -1),
            ("gx", "gy"),
            split_axis=0,
            concat_axis=0,
            tiled=True,
        ),
        lax.all_to_all(
            out_slots.reshape(devices, capacity),
            ("gx", "gy"),
            split_axis=0,
            concat_axis=0,
            tiled=True,
        ),
    )
    positions = line_count // segment
    placing = (
        arrived_slots.reshape(-1)[None, :] == jnp.arange(positions, dtype=jnp.int32)[:, None]
    ).astype(jnp.bfloat16)
    force_field = jnp.einsum(
        "pr,rxs->xps",
        placing,
        arrived.reshape(-1, cells_x, segment),
        preferred_element_type=jnp.float32,
    )
    right_side = velocity.reshape(cells_x, line_count) + force_field.reshape(cells_x, line_count)
    inner_rows = cells_x - 1
    below_diag = -viscosity
    above_diag = -viscosity
    main_diag = 1.0 + 2.0 * viscosity
    interior = thomas(
        below_diag[:inner_rows],
        main_diag[:inner_rows],
        above_diag[:inner_rows],
        right_side[:inner_rows],
    )
    unit_columns = (
        jnp.zeros((inner_rows, 2), jnp.float32).at[0, 0].add(1.0).at[inner_rows - 1, 1].add(1.0)
    )
    spikes = thomas(
        below_diag[:inner_rows], main_diag[:inner_rows], above_diag[:inner_rows], unit_columns
    )
    first_spike = spikes[:, 0]
    last_spike = spikes[:, 1]
    below_first = below_diag[0]
    above_inner = above_diag[inner_rows - 1]
    below_sep = below_diag[inner_rows]
    main_sep = main_diag[inner_rows]
    above_sep = above_diag[inner_rows]
    position = lax.axis_index("gx")
    handed = jnp.stack([below_first * first_spike[0], above_inner * last_spike[0]])
    next_first, next_scalars = passed_along((interior[0], handed), "gx", -1)
    lower_coef = jnp.where(
        position > 0, -below_sep * below_first * first_spike[inner_rows - 1], 0.0
    )
    center_coef = (
        main_sep
        - below_sep * above_inner * last_spike[inner_rows - 1]
        - above_sep * next_scalars[0]
    )
    upper_coef = -above_sep * next_scalars[1]
    reduced_side = (
        right_side[inner_rows] - below_sep * interior[inner_rows - 1] - above_sep * next_first
    )
    coefficients = jnp.stack([lower_coef, center_coef, upper_coef])
    split_coef = lax.all_gather(coefficients, "gx", axis=0, tiled=True).reshape(-1, 3)
    sides = lax.all_to_all(
        reduced_side.reshape(1, grid_x, -1), "gx", split_axis=1, concat_axis=0, tiled=True
    )[:, 0, :]
    separators = lax.linalg.tridiagonal_solve(
        split_coef[:, 0], split_coef[:, 1], split_coef[:, 2], sides
    )
    earlier = jnp.concatenate([jnp.zeros_like(separators[:1]), separators[:-1]], axis=0)
    solved_pairs = jnp.stack([separators, earlier])
    returned = lax.all_to_all(solved_pairs, "gx", split_axis=1, concat_axis=2, tiled=True)
    own_value = returned[0, 0]
    previous = returned[1, 0]
    inner_part = (
        interior
        - below_first * previous[None, :] * first_spike[:, None]
        - above_inner * own_value[None, :] * last_spike[:, None]
    )
    updated = jnp.concatenate([inner_part, own_value[None, :]], axis=0)
    return updated.reshape(velocity.shape)


def solution(mesh):
    placed = (
        P("gx", "gy", None),
        P("gx"),
        P(("gx", "gy"), None),
        P(("gx", "gy"), None, None),
        P(("gx", "gy"), None),
        P(("gx", "gy")),
    )
    return jax.shard_map(
        per_device, mesh=mesh, in_specs=placed, out_specs=P("gx", "gy", None), check_vma=False
    )
```

profile of v0, /device:TPU:0, one launch (start us, length us, event | category | flops | bytes accessed | tf_op | source)
XLA Modules:
  0.0 286.4 jit_solution(17958586952579366199)
XLA Ops:
  0.9 0.8 select_reduce_fusion.1
  2.4 0.8 convert_reduce_fusion
  3.9 7.3 %all-to-all-start.1 = ((s32[32,1,8]{2,1,0:T(1,128)}), s32[32,1,8]{2,1,0:T(1,128)S(1)}, u32[]{:S(2)}, u32[]{:S(2)}) async-start(s32[32,1,8]{2,1,0:T(1,128)} %bitcast.4), calls=%async_computation.1 | async-start | bytes 32768 | tf_op jit(solution)/shard_map/all_to_all | solution.py:63
  11.3 0.8 copy.18
  12.1 4.8 %fusion.70 = bf16[128,1,2048]{2,1,0:T(2,128)(2,1)S(1)} fusion(bf16[128,16,1]{1,2,0:T(2,128)(2,1)S(1)} %copy.18, bf16[128,16,2048]{2,1,0:T(8,128)(2,1)} %param.13), kind=kOutput, calls=%fused_computation.197 | convolution fusion | flops 8388608 | bytes 8916992 | tf_op jit(solution)/shard_map/bm,bmt->bt/dot_general | solution.py:34
  16.9 1.5 fusion
  18.4 5.8 %all-to-all-start = ((bf16[32,8,2048]{2,1,0:T(8,128)(2,1)}), bf16[32,8,2048]{2,1,0:T(8,128)(2,1)S(1)}, u32[]{:S(2)}, u32[]{:S(2)}) async-start(bf16[32,8,2048]{2,1,0:T(8,128)(2,1)} %fusion), calls=%async_computation | async-start | bytes 2097152 | tf_op jit(solution)/shard_map/all_to_all | solution.py:56
  52.6 8.7 %subtract_divide_fusion.29 = (f32[1,2]{0,1:T(2,128)S(1)}, f32[1,2]{0,1:T(2,128)S(1)}, f32[1,2]{0,1:T(2,128)S(1)}, f32[1,2]{0,1:T(2,128)S(1)}, f32[1,2]{0,1:T(2,1...) fusion(f32[]{:T(128)S(6)} %sub.3676, ...), kind=kLoop, calls=%fused_computation.160 | loop fusion | flops 80 | bytes 220 | tf_op jit(solution)/shard_map/div | solution.py:21
  61.3 1.2 multiply_subtract_fusion.31
  65.7 1.3 collective-permute-start.1
  68.7 6.6 %copy.20 = f32[2,8,128,512]{3,1,2,0:T(8,128)} copy(f32[2,8,128,512]{3,2,1,0:T(8,128)} %bitcast.267) | data formatting | bytes 8388608
  81.8 34.9 %all-reduce.1 = f32[48]{0:T(128)S(1)} all-reduce(f32[48]{0:T(128)S(1)} %maximum_dynamic-update-slice_fusion), channel_id=1, replica_groups=mesh['gx'=16,'gy'=2] {'gx'}, use_global_device_ids=true, to_apply=%add.1 | all-reduce | flops 48 | bytes 384
  149.3 2.7 convolution_bitcast_fusion
  152.1 5.3 %copy.16 = f32[16,512,128]{2,1,0:T(8,128)} copy(f32[16,512,128]{1,2,0:T(8,128)} %convolution_bitcast_fusion) | data formatting | bytes 8388608 | tf_op jit(solution)/shard_map/pr,rxs->xps/transpose | solution.py:75
  157.4 6.0 %bitcast_add_fusion = f32[16,65536]{1,0:T(8,128)S(1)} fusion(f32[16,65536]{1,0:T(8,128)} %bitcast.265, f32[2,8,512,128]{3,2,1,0:T(8,128)} %bitcast.266), kind=kLoop, calls=%fused_computation | loop fusion | flops 1048576 | bytes 12582912 | tf_op jit(solution)/shard_map/add | solution.py:81
  163.4 17.6 %fusion.39 = (f32[65536]{0:T(1024)}, f32[1,65536]{1,0:T(1,128)S(1)}, f32[1,65536]{1,0:T(1,128)S(1)}, f32[1,65536]{1,0:T(1,128)S(1)}, f32[1,65536]{1,0:T(1,128)S(...) fusion(f32[]{:T(128)S(6)} %div.2722, ...), kind=kLoop, calls=%fused_computation.181 | loop fusion | flops 2949120 | bytes 8126584 | tf_op jit(solution)/shard_map/sub | solution.py:24
  181.0 3.3 %fusion.61 = (f32[1,65536]{1,0:T(1,128)S(1)}, f32[1,65536]{1,0:T(1,128)S(1)}, f32[1,65536]{1,0:T(1,128)S(1)}, f32[1,65536]{1,0:T(1,128)S(1)}, f32[1,65536]{1,0:T...) fusion(f32[16,65536]{1,0:T(8,128)S(1)} %bitcast_add_fusion), kind=kLoop, calls=%fused_computation.188 | loop fusion | bytes 7864320 | tf_op jit(solution)/shard_map/slice | solution.py:118
  184.2 10.1 %multiply_subtract_fusion.2 = (f32[65536]{0:T(1024)}, f32[65536]{0:T(1024)}) fusion(f32[65536]{0:T(1024)S(1)} %bitcast.287, f32[]{:T(128)S(6)} %div.2722, f32[]{:T(128)S(6)} %div.2719, f32[]{:T(128)S(6)} %div.2716, f32[]{:T(128)S(6)} %div.2713, f32[]{:T(128)S(6)} %div.2710, f32[]{:T(128)S(6)} %div.2707, f32[]{:T(128)S(6)} %div.2704, f32[]{:T(128)S(6)} %div.2701, ...), kind=kLoop, calls=%fused_computation.16 | loop fusion | flops 4587520 | bytes 4456616 | tf_op jit(solution)/shard_map/sub | solution.py:24
  194.4 1.5 collective-permute-start
  195.9 1.8 fusion.40
  197.6 1.8 fusion.41
  199.4 1.8 fusion.42
  201.2 1.7 fusion.43
  202.9 1.8 fusion.44
  204.7 2.5 fusion.45
  207.2 1.7 stack.96
  208.9 1.7 constant_dynamic-update-slice_fusion.14
  210.6 1.7 stack.97
  212.3 1.7 stack.99
  214.0 1.7 stack.101
  215.7 1.7 stack.103
  217.3 1.7 stack.105
  219.1 1.7 constant_dynamic-update-slice_fusion.13
  220.7 1.7 constant_dynamic-update-slice_fusion.12
  222.4 1.7 constant_dynamic-update-slice_fusion.11
  224.8 1.7 constant_dynamic-update-slice_fusion.9
  226.5 6.2 %multiply_subtract_fusion.1 = f32[65536]{0:T(1024)} fusion(f32[65536]{0:T(1024)} %collective-permute-done, f32[65536]{0:T(1024)S(1)} %bitcast.289, f32[]{:T(128)} %bitcast.38, f32[]{:T(128)S(6)} %sub.3678, f32[65536]{0:T(1024)S(1)} %bitcast.271, f32[]{:T(128)S(6)} %sub.3676, f32[65536]{0:T(1024)S(1)} %bitcast.273, f32[]{:T(128)} %bitcast.33, f32[]{:T(128)} %bitcast.35, ...), kind=kLoop, calls=%fused_computation.15 | loop fusion | flops 1441792 | bytes 2621492 | tf_op jit(solution)/shard_map/sub | solution.py:118
  232.6 3.7 %all-to-all-start.2 = ((f32[1,16,4096]{2,0,1:T(1,128)}), f32[1,16,4096]{2,0,1:T(1,128)S(1)}, u32[]{:S(2)}, u32[]{:S(2)}) async-start(f32[1,16,4096]{2,0,1:T(1,128)} %bitcast.54), calls=%async_computation.2 | async-start | bytes 524288 | tf_op jit(solution)/shard_map/all_to_all | solution.py:122
  237.0 1.7 constant_dynamic-update-slice_fusion.7
  239.5 6.8 %all-to-all-done.2 = f32[1,16,4096]{2,0,1:T(1,128)S(1)} async-done(((f32[1,16,4096]{2,0,1:T(1,128)}), f32[1,16,4096]{2,0,1:T(1,128)S(1)}, u32[]{:S(2)}, u32[]{:S(2)}) %all-to-all-start.2) | async-done | bytes 262176 | tf_op jit(solution)/shard_map/all_to_all | solution.py:122
  246.3 9.5 %fusion.11 = (f32[1,4096]{1,0:T(1,128)S(1)}, f32[1,4096]{1,0:T(1,128)S(1)}, f32[1,4096]{1,0:T(1,128)S(1)}, f32[1,4096]{1,0:T(1,128)S(1)}, f32[1,4096]{1,0:T(1,12...) fusion(f32[1,16,4096]{2,0,1:T(1,128)S(1)} %all-to-all-done.2, ...), kind=kLoop, calls=%fused_computation.88 | loop fusion | flops 176128 | bytes 491636 | tf_op jit(solution)/shard_map/eval_jaxpr/div | solution.py:125
  255.7 0.9 multiply_subtract_fusion.16
  258.0 1.3 pad_maximum_fusion.1
  259.3 3.8 %all-to-all-start.3 = ((f32[2,16,4096]{2,0,1:T(2,128)}), f32[2,16,4096]{2,0,1:T(2,128)S(1)}, u32[]{:S(2)}, u32[]{:S(2)}) async-start(f32[2,16,4096]{2,0,1:T(2,128)} %pad_maximum_fusion.1), calls=%async_computation.3 | async-start | bytes 1048576 | tf_op jit(solution)/shard_map/all_to_all | solution.py:130
  267.6 9.5 %all-to-all-done.3 = f32[2,16,4096]{2,0,1:T(2,128)S(1)} async-done(((f32[2,16,4096]{2,0,1:T(2,128)}), f32[2,16,4096]{2,0,1:T(2,128)S(1)}, u32[]{:S(2)}, u32[]{:S(2)}) %all-to-all-start.3) | async-done | bytes 524320 | tf_op jit(solution)/shard_map/all_to_all | solution.py:130
  277.1 3.2 %fusion.4 = (f32[16,4096]{1,0:T(8,128)S(1)}, f32[16,4096]{1,0:T(8,128)S(1)}, f32[16,4096]{1,0:T(8,128)S(1)}) fusion(f32[2,16,4096]{2,0,1:T(2,128)S(1)} %all-to-all-done.3, f32[]{:T(128)} %bitcast.8, f32[]{:T(128)} %bitcast.35), kind=kLoop, calls=%fused_computation.12 | loop fusion | flops 131072 | bytes 1310728 | tf_op jit(solution)/shard_map/mul | solution.py:135
  280.5 3.2 %multiply_subtract_fusion = f32[15,128,512]{2,1,0:T(8,128)S(1)} fusion(f32[15,128,512]{2,1,0:T(8,128)} %constant_dynamic-update-slice_fusion, f32[15]{0:T(128)S(1)} %get-tuple-element.186, f32[128,512]{1,0:T(8,128)S(1)} %mul.4323, f32[15]{0:T(128)S(1)} %get-tuple-element.185, f32[128,512]{1,0:T(8,128)S(1)} %mul.4316), kind=kLoop, calls=%fused_computation.2 | loop fusion | flops 3932160 | bytes 8388728 | tf_op jit(solution)/shard_map/sub | solution.py:134
  283.7 2.7 pad_maximum_fusion
  (61 shorter events, 17.9 us)
Async XLA Ops:
  3.9 14.5 %all-to-all-start.1 = ((s32[32,1,8]{2,1,0:T(1,128)}), s32[32,1,8]{2,1,0:T(1,128)S(1)}, u32[]{:S(2)}, u32[]{:S(2)}) async-start(s32[32,1,8]{2,1,0:T(1,128)} %bitcast.4), calls=%async_computation.1 | async-start | bytes 32768 | tf_op jit(solution)/shard_map/all_to_all | solution.py:63
  12.1 12.2 %copy-start.5 = (f32[16]{0:T(128)S(1)}, f32[16]{0:T(128)}, u32[]{:S(2)}) copy-start(f32[16]{0:T(128)} %param.11) | copy-start | bytes 196
  12.1 40.5 %copy-start.3 = (f32[1,2]{0,1:T(2,128)S(1)}, f32[1,2]{0,1:T(2,128)}, u32[]{:S(2)}) copy-start(f32[1,2]{0,1:T(2,128)} %constant.203.clone.1) | copy-start | bytes 28
  16.9 44.4 %copy-start.4 = (f32[1,2]{0,1:T(2,128)S(1)}, f32[1,2]{0,1:T(2,128)}, u32[]{:S(2)}) copy-start(f32[1,2]{0,1:T(2,128)} %constant.201.clone.1) | copy-start | bytes 28
  18.4 130.7 %all-to-all-start = ((bf16[32,8,2048]{2,1,0:T(8,128)(2,1)}), bf16[32,8,2048]{2,1,0:T(8,128)(2,1)S(1)}, u32[]{:S(2)}, u32[]{:S(2)}) async-start(bf16[32,8,2048]{2,1,0:T(8,128)(2,1)} %fusion), calls=%async_computation | async-start | bytes 2097152 | tf_op jit(solution)/shard_map/all_to_all | solution.py:56
  65.7 13.4 %collective-permute-start.1 = (f32[2]{0:T(128)S(1)}, f32[2]{0:T(128)S(1)}, u32[]{:S(2)}, u32[]{:S(2)}) collective-permute-start(f32[2]{0:T(128)S(1)} %pad_maximum_fusion.2), channel_id=1, source_target_pairs={{2,0},{4,2},{6,4},{8,6},{10,8},{12,10},{14,12},{16,14},{18,16},{20... | collective-permute-start | bytes 32 | tf_op jit(solution)/shard_map/ppermute | solution.py:10
  68.7 7.3 %copy-start.6 = (u32[32]{0:T(128)S(1)}, u32[32]{0:T(128)}, u32[]{:S(2)}) copy-start(u32[32]{0:T(128)} %constant.208) | copy-start | bytes 388
  194.4 32.1 %collective-permute-start = (f32[65536]{0:T(1024)}, f32[65536]{0:T(1024)}, u32[]{:S(2)}, u32[]{:S(2)}) collective-permute-start(f32[65536]{0:T(1024)} %get-tuple-element.122), channel_id=1, source_target_pairs={{2,0},{4,2},{6,4},{8,6},{10,8},{12,10},{14,12},{16,14},{18,16},{20... | collective-permute-start | bytes 786440 | tf_op jit(solution)/shard_map/ppermute | solution.py:10
  232.6 30.5 %copy-start.1 = (f32[1,128,512]{2,1,0:T(8,128)S(1)}, f32[1,128,512]{2,1,0:T(8,128)}, u32[]{:S(2)}) copy-start(f32[1,128,512]{2,1,0:T(8,128)} %stack.105) | copy-start | bytes 786436
  232.6 13.6 %all-to-all-start.2 = ((f32[1,16,4096]{2,0,1:T(1,128)}), f32[1,16,4096]{2,0,1:T(1,128)S(1)}, u32[]{:S(2)}, u32[]{:S(2)}) async-start(f32[1,16,4096]{2,0,1:T(1,128)} %bitcast.54), calls=%async_computation.2 | async-start | bytes 524288 | tf_op jit(solution)/shard_map/all_to_all | solution.py:122
  236.3 27.6 %copy-start = (f32[65536]{0:T(1024)S(1)}, f32[65536]{0:T(1024)}, u32[]{:S(2)}) copy-start(f32[65536]{0:T(1024)} %get-tuple-element.52) | copy-start | bytes 786436
  237.0 26.9 %copy-start.2 = (f32[65536]{0:T(1024)S(1)}, f32[65536]{0:T(1024)}, u32[]{:S(2)}) copy-start(f32[65536]{0:T(1024)} %get-tuple-element.36) | copy-start | bytes 786436
  259.3 17.8 %all-to-all-start.3 = ((f32[2,16,4096]{2,0,1:T(2,128)}), f32[2,16,4096]{2,0,1:T(2,128)S(1)}, u32[]{:S(2)}, u32[]{:S(2)}) async-start(f32[2,16,4096]{2,0,1:T(2,128)} %pad_maximum_fusion.1), calls=%async_computation.3 | async-start | bytes 1048576 | tf_op jit(solution)/shard_map/all_to_all | solution.py:130
where the time goes:
time: 289 us; the launch traced here: 286 us
  other arithmetic  86 us (30%)
  between operations  65.1 us (23%)
  local copies, waits for them, and re-layouts  51.5 us (18%)
  blocking collectives  34.9 us (12%)
  starting transfers between devices  23.4 us (8%)
  waiting for transfers between devices  16.3 us (6%)
  matrix products  9.06 us (3%)
    sub x9, other arithmetic, thomas(): result.append(values[row_index] - ratios[row_index] * result[-1])  40.2 us
    unnamed x1, blocking collectives  34.9 us
    unnamed x33, local copies, waits for them, and re-layouts  24.1 us
    another operation x10, local copies, waits for them, and re-layouts, thomas(): return jnp.stack(result[::-1])  11.1 us
    all_to_all x1, waiting for transfers between devices, per_device(): lax.all_to_all(solved_pairs, 'gx', split_axis=1, concat_axis=2, tiled=True)  9.53 us
    div x1, other arithmetic, per_device(): lax.linalg.tridiagonal_solve(split_coef[:, 0], split_coef[:, 1], split_co...  9.47 us
    div x1, other arithmetic, thomas(): (right_side[row_index] - below_diag[row_index] * values[-1]) / pivot_value  8.72 us
    all_to_all x1, starting transfers between devices, per_device(): lax.all_to_all(out_slots.reshape(devices, capacity), ('gx', 'gy'), split_...  7.33 us
  transfers between devices with their start and end apart: 6, of which 2 were waited for; matrix products, arithmetic and copies ran while one was open for 24% of the time, Pallas kernels for 0%

commit v1 on v0

v1 whole, which is shorter than its diff:
```python
import functools

import jax
import jax.numpy as jnp
from jax import lax
from jax.experimental import pallas as pl
from jax.experimental.pallas import tpu as pltpu
from jax.sharding import PartitionSpec as P

F32 = jnp.float32
BF16 = jnp.bfloat16
BASE = 256


def iota(shape, axis):
    return lax.broadcasted_iota(jnp.int32, shape, axis)


def nt_dot(a, b):
    return lax.dot_general(a, b, (((1,), (1,)), ((), ())), preferred_element_type=F32)


def spread_kernel(devices, capacity, f_ref, w_ref, owner_ref, slot_ref, out_ref, tiles_ref):
    step = pl.program_id(0)
    group, markers = f_ref.shape
    cells = w_ref.shape[2]
    wide = group * markers
    pick = (iota((markers, wide), 1) % markers == iota((markers, wide), 0)).astype(BF16)
    tiled = jnp.dot(f_ref[...], pick, preferred_element_type=F32)
    block = iota((group, wide), 1) // markers == iota((group, wide), 0)
    forces = jnp.where(block, tiled, 0.0).astype(BF16)
    weights = w_ref[...].reshape(wide, cells)
    tiles = jnp.dot(forces, weights, preferred_element_type=F32).astype(BF16)
    tiles_ref[pl.ds(pl.multiple_of(step * group, group), group), :] = tiles

    @pl.when(step == pl.num_programs(0) - 1)
    def _():
        blocks = owner_ref.shape[1]
        rows = devices * capacity
        owner = owner_ref[...]
        matches = (iota((devices, blocks), 0) == owner).astype(F32)
        earlier = (iota((blocks, blocks), 0) < iota((blocks, blocks), 1)).astype(BF16)
        counts = jnp.dot(matches.astype(BF16), earlier, preferred_element_type=F32)
        rank = jnp.sum(counts * matches, axis=0, keepdims=True).astype(jnp.int32)
        target = owner * capacity + rank
        select = (iota((rows, blocks), 0) == target).astype(BF16)
        out = jnp.dot(select, tiles_ref[...], preferred_element_type=F32)
        number = slot_ref[...] + 1
        lane = iota((128, blocks), 0)
        digits = jnp.where(lane == 0, number // BASE, jnp.where(lane == 1, number % BASE, 0))
        meta = nt_dot(select, digits.astype(F32).astype(BF16))
        if capacity % 8 == 0:
            out_ref[:, :, :cells] = out.reshape(devices, capacity, cells).astype(BF16)
            out_ref[:, :, cells:] = meta.reshape(devices, capacity, 128).astype(BF16)
        else:
            for d in range(devices):
                lo, hi = d * capacity, (d + 1) * capacity
                out_ref[d, :, :cells] = out[lo:hi].astype(BF16)
                out_ref[d, :, cells:] = meta[lo:hi].astype(BF16)


def spread(forces, weights, owner, slots, devices, capacity):
    blocks, markers, cells = weights.shape
    group = min(blocks, max(8, 256 // markers))
    return pl.pallas_call(
        functools.partial(spread_kernel, devices, capacity),
        out_shape=jax.ShapeDtypeStruct((devices, capacity, cells + 128), BF16),
        grid=(blocks // group,),
        in_specs=[
            pl.BlockSpec((group, markers), lambda i: (i, 0)),
            pl.BlockSpec((group, markers, cells), lambda i: (i, 0, 0)),
            pl.BlockSpec((1, blocks), lambda i: (0, 0)),
            pl.BlockSpec((1, blocks), lambda i: (0, 0)),
        ],
        out_specs=pl.BlockSpec((devices, capacity, cells + 128), lambda i: (0, 0, 0)),
        scratch_shapes=[pltpu.VMEM((blocks, cells), BF16)],
        compiler_params=pltpu.CompilerParams(vmem_limit_bytes=24 << 20),
        cost_estimate=pl.CostEstimate(
            flops=2 * blocks * markers * cells * 64, bytes_accessed=weights.size * 2, transcendentals=0
        ),
    )(forces, weights, owner, slots)


def factor(visc):
    inverse, ratio = [], []
    for x in range(len(visc) - 1):
        pivot = 1.0 + 2.0 * visc[x]
        if x:
            pivot = pivot - visc[x] * ratio[-1]
        inverse.append(1.0 / pivot)
        ratio.append(visc[x] * inverse[-1])
    return inverse, ratio


def spikes(inverse, ratio):
    count = len(inverse)
    left = [inverse[0]]
    for x in range(1, count):
        left.append(ratio[x] * left[-1])
    for x in range(count - 2, -1, -1):
        left[x] = left[x] + ratio[x] * left[x + 1]
    right = [inverse[-1]]
    for x in range(count - 2, -1, -1):
        right.append(ratio[x] * right[-1])
    return left, right[::-1]


def local_kernel(visc_ref, velocity_ref, arrived_ref, out_ref, ends_ref, rhs_ref, coef_ref, flat_ref):
    cells_x, rows_y, seg = velocity_ref.shape
    devices, capacity, width = arrived_ref.shape
    rows = devices * capacity
    cells = width - 128
    segments = pl.num_programs(0)
    z = pl.program_id(0)

    @pl.when(z == 0)
    def _():
        visc = [jnp.full((8, seg), visc_ref[x], F32) for x in range(cells_x)]
        inverse, ratio = factor(visc)
        for x in range(cells_x - 1):
            coef_ref[x] = inverse[x]
            coef_ref[cells_x + x] = ratio[x]
        coef_ref[cells_x - 1] = visc[-1]
        if capacity % 8 == 0:
            flat_ref[...] = arrived_ref[...].astype(F32).reshape(rows, width).astype(BF16)
        else:
            parts = [arrived_ref[d].astype(F32) for d in range(devices)]
            flat_ref[...] = jnp.concatenate(parts, axis=0).astype(BF16)

    lane = iota((8, 128), 1)
    base = jnp.where(lane == 0, float(BASE), jnp.where(lane == 1, 1.0, 0.0)).astype(BF16)
    number = nt_dot(base, flat_ref[:, cells:])[0:1, :].astype(jnp.int32) - 1
    place = (iota((rows_y, rows), 0) * segments + z == number).astype(BF16)
    rhs_ref[...] = jnp.dot(place, flat_ref[:, :cells], preferred_element_type=F32)

    def chunk(i, carry):
        at = pl.ds(pl.multiple_of(i * 8, 8), 8)

        def side(x):
            return velocity_ref[x, at, :] + rhs_ref[at, x * seg : (x + 1) * seg]

        values = [side(0) * coef_ref[0]]
        for x in range(1, cells_x - 1):
            values.append(side(x) * coef_ref[x] + coef_ref[cells_x + x] * values[-1])
        last = cells_x - 1
        ends_ref[0, at, :] = side(last) + coef_ref[last] * values[-1]
        value = values[-1]
        out_ref[last - 1, at, :] = value
        for x in range(last - 2, -1, -1):
            value = values[x] + coef_ref[cells_x + x] * value
            out_ref[x, at, :] = value
        ends_ref[1, at, :] = value
        return carry

    lax.fori_loop(0, rows_y // 8, chunk, 0, unroll=2)


def local_solve(viscosity, velocity, arrived, seg):
    cells_x, cells_y, cells_z = velocity.shape
    devices, capacity, width = arrived.shape
    rows = devices * capacity
    return pl.pallas_call(
        local_kernel,
        out_shape=(
            jax.ShapeDtypeStruct((cells_x - 1, cells_y, cells_z), F32),
            jax.ShapeDtypeStruct((2, cells_y, cells_z), F32),
        ),
        grid=(cells_z // seg,),
        in_specs=[
            pl.BlockSpec(memory_space=pltpu.SMEM),
            pl.BlockSpec((cells_x, cells_y, seg), lambda i: (0, 0, i)),
            pl.BlockSpec((devices, capacity, width), lambda i: (0, 0, 0)),
        ],
        out_specs=(
            pl.BlockSpec((cells_x - 1, cells_y, seg), lambda i: (0, 0, i)),
            pl.BlockSpec((2, cells_y, seg), lambda i: (0, 0, i)),
        ),
        scratch_shapes=[
            pltpu.VMEM((cells_y, cells_x * seg), F32),
            pltpu.VMEM((2 * cells_x, 8, seg), F32),
            pltpu.VMEM((rows, width), BF16),
        ],
        compiler_params=pltpu.CompilerParams(vmem_limit_bytes=24 << 20),
    )(viscosity, velocity, arrived)


def couple_kernel(visc_ref, out_ref):
    cells_x, count, lanes = visc_ref.shape
    visc = [visc_ref[x] for x in range(cells_x)]
    inverse, ratio = factor(visc)
    left, right = spikes(inverse, ratio)
    row = iota((count, lanes), 0)

    def following(value):
        moved = jnp.concatenate([value[1:], value[:1]], axis=0)
        return jnp.where(row == count - 1, 0.0, moved)

    sep, inner, first = visc[-1], visc[-2], visc[0]
    lower = jnp.where(row > 0, -sep * first * left[-1], 0.0)
    center = 1.0 + 2.0 * sep - sep * inner * right[-1] - sep * following(first * left[0])
    upper = -sep * following(inner * right[0])
    previous = jnp.zeros((1, lanes), F32)
    for d in range(count):
        pivot = center[d : d + 1] - lower[d : d + 1] * previous
        inv = 1.0 / pivot
        previous = upper[d : d + 1] * inv
        out_ref[0, d : d + 1, :] = inv
        out_ref[1, d : d + 1, :] = previous
    out_ref[2] = lower
    out_ref[3] = jnp.where(row == count - 1, 0.0, sep)


def couple(splat):
    return pl.pallas_call(
        couple_kernel,
        out_shape=jax.ShapeDtypeStruct((4,) + splat.shape[1:], F32),
    )(splat)


def reduced_kernel(coef_ref, sides_ref, out_ref):
    count, rows, cells_z = sides_ref.shape[1:]
    lanes = coef_ref.shape[2]
    for c in range(cells_z // lanes):
        at = slice(c * lanes, (c + 1) * lanes)
        values = []
        for d in range(count):
            side = sides_ref[0, d, :, at]
            if d + 1 < count:
                side = side + coef_ref[3, d : d + 1, :] * sides_ref[1, d + 1, :, at]
            if d:
                side = side - coef_ref[2, d : d + 1, :] * values[-1]
            values.append(side * coef_ref[0, d : d + 1, :])
        value = values[-1]
        out_ref[0, count - 1, :, at] = value
        for d in range(count - 2, -1, -1):
            value = values[d] - coef_ref[1, d : d + 1, :] * value
            out_ref[0, d, :, at] = value
            out_ref[1, d + 1, :, at] = value
        out_ref[1, 0, :, at] = jnp.zeros_like(value)


def reduced(coefs, sides):
    return pl.pallas_call(
        reduced_kernel,
        out_shape=jax.ShapeDtypeStruct(sides.shape, F32),
    )(coefs, sides)


def final_kernel(visc_ref, inner_ref, ends_ref, out_ref, coef_ref):
    count, rows_y, cells_z = inner_ref.shape
    seg = coef_ref.shape[2]

    @pl.when(pl.program_id(0) == 0)
    def _():
        visc = [jnp.full((8, seg), visc_ref[x], F32) for x in range(count + 1)]
        left, right = spikes(*factor(visc))
        for x in range(count):
            coef_ref[x] = visc[0] * left[x]
            coef_ref[count + x] = visc[count - 1] * right[x]

    def chunk(i, carry):
        at = pl.ds(pl.multiple_of(i * 8, 8), 8)
        for c in range(cells_z // seg):
            lane = slice(c * seg, (c + 1) * seg)
            own, before = ends_ref[0, at, lane], ends_ref[1, at, lane]
            for x in range(count):
                out_ref[x, at, lane] = (
                    inner_ref[x, at, lane] + coef_ref[x] * before + coef_ref[count + x] * own
                )
            out_ref[count, at, lane] = own
        return carry

    lax.fori_loop(0, rows_y // 8, chunk, 0)


def final(viscosity, inner, ends, seg):
    count, cells_y, cells_z = inner.shape
    parts = 4
    rows = cells_y // parts
    return pl.pallas_call(
        final_kernel,
        out_shape=jax.ShapeDtypeStruct((count + 1, cells_y, cells_z), F32),
        grid=(parts,),
        in_specs=[
            pl.BlockSpec(memory_space=pltpu.SMEM),
            pl.BlockSpec((count, rows, cells_z), lambda i: (0, i, 0)),
            pl.BlockSpec((2, rows, cells_z), lambda i: (0, i, 0)),
        ],
        out_specs=pl.BlockSpec((count + 1, rows, cells_z), lambda i: (0, i, 0)),
        scratch_shapes=[pltpu.VMEM((2 * count, 8, seg), F32)],
        compiler_params=pltpu.CompilerParams(vmem_limit_bytes=24 << 20),
    )(viscosity, inner, ends)


def per_device(velocity, viscosity, marker_forces, spread_weights, block_owner, tile_slot):
    cells_x, cells_y, cells_z = velocity.shape
    grid_x = lax.axis_size("gx")
    devices = grid_x * lax.axis_size("gy")
    blocks, _, cells = spread_weights.shape
    capacity = max(2, 2 * blocks // devices)
    seg = cells // cells_x
    whole = lax.all_gather(viscosity, "gx", axis=0, tiled=True).reshape(grid_x, cells_x)
    splat = jnp.broadcast_to(whole.T[:, :, None], (cells_x, grid_x, 128))
    outgoing = spread(
        marker_forces,
        spread_weights,
        block_owner.reshape(1, blocks),
        tile_slot.reshape(1, blocks),
        devices,
        capacity,
    )
    arrived = lax.all_to_all(outgoing, ("gx", "gy"), split_axis=0, concat_axis=0, tiled=True)
    coefs = couple(splat)
    inner, ends = local_solve(viscosity, velocity, arrived, seg)
    sides = lax.all_to_all(
        ends.reshape(2, grid_x, -1, cells_z), "gx", split_axis=1, concat_axis=1, tiled=True
    )
    returned = lax.all_to_all(reduced(coefs, sides), "gx", split_axis=1, concat_axis=1, tiled=True)
    return final(viscosity, inner, returned.reshape(2, cells_y, cells_z), seg)


def solution(mesh):
    placed = (
        P("gx", "gy", None),
        P("gx"),
        P(("gx", "gy"), None),
        P(("gx", "gy"), None, None),
        P(("gx", "gy"), None),
        P(("gx", "gy")),
    )
    return jax.shard_map(
        per_device, mesh=mesh, in_specs=placed, out_specs=P("gx", "gy", None), check_vma=False
    )
```

time: 289 us -> 124 us (0.43)
  other arithmetic: 86 us -> 0 us
  between operations: 65.1 us -> 0.72 us
  blocking collectives: 34.9 us -> 88.3 us
  local copies, waits for them, and re-layouts: 51.5 us -> 14.1 us
  starting transfers between devices: 23.4 us -> 3.57 us
  Pallas kernels: 0 us -> 16.6 us
  waiting for transfers between devices: 16.3 us -> 0.01 us
  matrix products: 9.06 us -> 0 us
    all_to_all x0 -> x2, blocking collectives: none -> 53.1 us  [the longest x1 36.2 us: per_device(): lax.all_to_all(outgoing, ('gx', 'gy'), split_axis=0, concat_axis=0, tiled...]
    sub x13 -> x0, other arithmetic: 50.4 us -> none  [the longest x9 40.2 us: thomas(): result.append(values[row_index] - ratios[row_index] * result[-1])]
    div x2 -> x0, other arithmetic: 18.2 us -> none  [the longest x1 9.47 us: per_device(): lax.linalg.tridiagonal_solve(split_coef[:, 0], split_coef[:, 1], split_co...]
    all_to_all x4 -> x1, starting transfers between devices: 20.7 us -> 3.57 us  [per_device(): lax.all_to_all(ends.reshape(2, grid_x, -1, cells_z), 'gx', split_axis=1,...]
    pallas_call x0 -> x5, Pallas kernels: none -> 16.6 us  [the longest x1 6 us: local_solve(): pl.pallas_call(local_kernel, out_shape=(jax.ShapeDtypeStruct((cells_x - 1...]
    all_to_all x4 -> x1, waiting for transfers between devices: 16.3 us -> 0.01 us  [per_device(): lax.all_to_all(ends.reshape(2, grid_x, -1, cells_z), 'gx', split_axis=1,...]
    unnamed x33 -> x20, local copies, waits for them, and re-layouts: 24.1 us -> 10.4 us
    another operation x12 -> x0, local copies, waits for them, and re-layouts: 11.6 us -> none  [the longest x10 11.1 us: thomas(): return jnp.stack(result[::-1])]
  transfers between devices with their start and end apart: 6 -> 1, of which waited for: 2 -> 0; matrix products, arithmetic and copies ran while one was open for 24% -> 1% of each run, Pallas kernels for 0% -> 1%
where the time goes in v1:
time: 124 us; the launch traced here: 123 us
  blocking collectives  88.3 us (71%)
  Pallas kernels  16.6 us (13%)
  local copies, waits for them, and re-layouts  14.1 us (11%)
  starting transfers between devices  3.57 us (3%)
    all_to_all x1, blocking collectives, per_device(): lax.all_to_all(outgoing, ('gx', 'gy'), split_axis=0, concat_axis=0, tiled...  36.2 us
    unnamed x1, blocking collectives  35.1 us
    all_to_all x1, blocking collectives, per_device(): lax.all_to_all(reduced(coefs, sides), 'gx', split_axis=1, concat_axis=1,...  16.9 us
    unnamed x20, local copies, waits for them, and re-layouts  10.4 us
    pallas_call x1, Pallas kernels, local_solve(): pl.pallas_call(local_kernel, out_shape=(jax.ShapeDtypeStruct((cells_x - 1...  6 us
    all_to_all x1, starting transfers between devices, per_device(): lax.all_to_all(ends.reshape(2, grid_x, -1, cells_z), 'gx', split_axis=1,...  3.57 us
    pallas_call x1, Pallas kernels, final(): pl.pallas_call(final_kernel, out_shape=jax.ShapeDtypeStruct((count + 1, c...  3.51 us
    pallas_call x1, Pallas kernels, spread(): pl.pallas_call(functools.partial(spread_kernel, devices, capacity), out_s...  3.24 us
  transfers between devices with their start and end apart: 1, of which 0 were waited for; matrix products, arithmetic and copies ran while one was open for 1% of the time, Pallas kernels for 1%

profile of v1, /device:TPU:0, one launch (start us, length us, event | category | flops | bytes accessed | tf_op | source)
XLA Modules:
  0.0 123.3 jit_solution(2650062766599272549)
XLA Ops:
  0.0 0.8 copy.10.f_ref
  0.8 0.0 copy-start
  0.8 3.4 %copy-done = bf16[128,16,2048]{2,1,0:T(8,128)(2,1)S(1)} copy-done((bf16[128,16,2048]{2,1,0:T(8,128)(2,1)S(1)}, bf16[128,16,2048]{2,1,0:T(8,128)(2,1)}, u32[]{:S(2)}) %copy-start) | copy-done | bytes 8388632
  4.2 0.0 copy-start.5
  4.2 0.7 copy-done.5
  4.8 0.0 copy-start.6
  4.8 0.7 copy-done.6
  5.5 0.0 copy-start.1
  5.5 0.0 copy-start.4
  5.5 3.2 %shard_map.64 = bf16[32,8,2176]{2,1,0:T(8,128)(2,1)S(1)} custom-call(bf16[128,16]{1,0:T(8,128)(2,1)S(1)} %copy.10.f_ref, bf16[128,16,2048]{2,1,0:T(8,128)(2,1)S(1)} %copy-done, s32[1,128]{1,0:T(1,128)S(1)} %bitcast.10, s32[1,128]{1,0:T(1,128)S(1)} %bitcast.11), custom_call_target="tpu_custom_call" | custom-call | flops 536870912 | bytes 8388608 | tf_op jit(solution)/shard_map/pallas_call | solution.py:65
  8.7 36.2 %all_to_all.15.arrived_ref = bf16[32,8,2176]{2,1,0:T(8,128)(2,1)S(1)} all-to-all(bf16[32,8,2176]{2,1,0:T(8,128)(2,1)S(1)} %shard_map.64), channel_id=1, replica_groups=mesh['gx'=16,'gy'=2] {'gx','gy'}, dimensions={0} | all-to-all | bytes 2228224 | tf_op jit(solution)/shard_map/all_to_all | solution.py:312
  45.0 0.0 copy-done.1
  45.0 0.0 copy-done.4
  45.0 0.0 copy-start.7
  45.0 6.0 %shard_map.65 = (f32[15,128,512]{2,1,0:T(8,128)S(1)}, f32[2,128,512]{2,1,0:T(8,128)S(1)}) custom-call(f32[16]{0:T(128)S(1)} %copy-done.4, f32[16,128,512]{2,1,0:T(8,128)S(1)} %copy-done.1, bf16[32,8,2176]{2,1,0:T(8,128)(2,1)S(1)} %all_to_all.15.arrived_ref), custom_call_target="tpu_custom_call" | custom-call | tf_op jit(solution)/shard_map/pallas_call | solution.py:162
  51.0 0.0 copy-start.2
  51.0 1.9 %copy-done.2 = f32[15,128,512]{2,1,0:T(8,128)} copy-done((f32[15,128,512]{2,1,0:T(8,128)}, f32[15,128,512]{2,1,0:T(8,128)S(1)}, u32[]{:S(2)}) %copy-start.2) | copy-done | bytes 3932184
  52.9 0.8 copy.12
  53.8 3.6 %all-to-all-start.1 = ((f32[2,16,8,512]{3,2,0,1:T(8,128)}), f32[2,16,8,512]{3,2,0,1:T(8,128)S(1)}, u32[]{:S(2)}, u32[]{:S(2)}) async-start(f32[2,16,8,512]{3,2,0,1:T(8,128)} %copy.12), calls=%async_computation.1 | async-start | bytes 1048576 | tf_op jit(solution)/shard_map/all_to_all | solution.py:315
  57.4 0.0 copy-done.7
  57.4 0.6 dynamic-slice
  58.6 0.2 dynamic-update-slice
  58.9 35.1 %all-reduce = f32[256]{0:T(256)S(1)} all-reduce(f32[256]{0:T(256)S(1)} %dynamic-update-slice), channel_id=1, replica_groups=mesh['gx'=16,'gy'=2] {'gx'}, use_global_device_ids=true, to_apply=%add | all-reduce | flops 256 | bytes 2048
  94.0 0.1 reshape.18
  94.1 0.1 copy.11
  94.2 0.8 broadcast_in_dim.2.visc_ref
  94.9 1.8 %shard_map.66.coef_ref = f32[4,16,128]{2,1,0:T(8,128)} custom-call(f32[16,16,128]{2,1,0:T(8,128)} %broadcast_in_dim.2.visc_ref), custom_call_target="tpu_custom_call" | custom-call | tf_op jit(solution)/shard_map/pallas_call | solution.py:214
  96.8 0.0 all-to-all-done.1
  96.8 0.8 copy.13.sides_ref
  97.6 2.0 %shard_map.67 = f32[2,16,8,512]{3,2,1,0:T(8,128)} custom-call(f32[4,16,128]{2,1,0:T(8,128)} %shard_map.66.coef_ref, f32[2,16,8,512]{3,2,1,0:T(8,128)} %copy.13.sides_ref), custom_call_target="tpu_custom_call" | custom-call | tf_op jit(solution)/shard_map/pallas_call | solution.py:243
  99.6 1.1 copy.14
  100.7 16.9 %all_to_all.16 = f32[2,16,8,512]{3,2,0,1:T(8,128)S(1)} all-to-all(f32[2,16,8,512]{3,2,0,1:T(8,128)S(1)} %copy.14), channel_id=1, replica_groups=mesh['gx'=16,'gy'=2] {'gx'}, dimensions={1} | all-to-all | bytes 1048576 | tf_op jit(solution)/shard_map/all_to_all | solution.py:318
  117.6 0.0 copy-start.3
  117.6 2.1 %copy-done.3 = f32[15,128,512]{2,1,0:T(8,128)S(1)} copy-done((f32[15,128,512]{2,1,0:T(8,128)S(1)}, f32[15,128,512]{2,1,0:T(8,128)}, u32[]{:S(2)}) %copy-start.3) | copy-done | bytes 3932184
  119.8 3.5 %shard_map.68 = f32[16,128,512]{2,1,0:T(8,128)} custom-call(f32[16]{0:T(128)S(1)} %copy-done.4, f32[15,128,512]{2,1,0:T(8,128)S(1)} %copy-done.3, f32[2,128,512]{2,1,0:T(8,128)S(1)} %bitcast.8), custom_call_target="tpu_custom_call" | custom-call | tf_op jit(solution)/shard_map/pallas_call | solution.py:280
  (2 shorter events, 0.0 us)
Async XLA Ops:
  0.8 3.4 %copy-start = (bf16[128,16,2048]{2,1,0:T(8,128)(2,1)S(1)}, bf16[128,16,2048]{2,1,0:T(8,128)(2,1)}, u32[]{:S(2)}) copy-start(bf16[128,16,2048]{2,1,0:T(8,128)(2,1)} %w_ref.1) | copy-start | bytes 25165828
  4.2 0.7 copy-start.5
  4.8 0.7 copy-start.6
  5.5 39.5 %copy-start.1 = (f32[16,128,512]{2,1,0:T(8,128)S(1)}, f32[16,128,512]{2,1,0:T(8,128)}, u32[]{:S(2)}) copy-start(f32[16,128,512]{2,1,0:T(8,128)} %velocity_ref.1) | copy-start | bytes 12582916
  5.5 39.5 %copy-start.4 = (f32[16]{0:T(128)S(1)}, f32[16]{0:T(128)}, u32[]{:S(2)}) copy-start(f32[16]{0:T(128)} %visc_ref.3) | copy-start | bytes 196
  45.0 12.4 %copy-start.7 = (u32[32]{0:T(128)S(1)}, u32[32]{0:T(128)}, u32[]{:S(2)}) copy-start(u32[32]{0:T(128)} %constant.2) | copy-start | bytes 388
  51.0 1.9 %copy-start.2 = (f32[15,128,512]{2,1,0:T(8,128)}, f32[15,128,512]{2,1,0:T(8,128)S(1)}, u32[]{:S(2)}) copy-start(f32[15,128,512]{2,1,0:T(8,128)S(1)} %get-tuple-element.7.inner_ref) | copy-start | bytes 11796484
  53.8 43.0 %all-to-all-start.1 = ((f32[2,16,8,512]{3,2,0,1:T(8,128)}), f32[2,16,8,512]{3,2,0,1:T(8,128)S(1)}, u32[]{:S(2)}, u32[]{:S(2)}) async-start(f32[2,16,8,512]{3,2,0,1:T(8,128)} %copy.12), calls=%async_computation.1 | async-start | bytes 1048576 | tf_op jit(solution)/shard_map/all_to_all | solution.py:315
  117.6 2.1 %copy-start.3 = (f32[15,128,512]{2,1,0:T(8,128)S(1)}, f32[15,128,512]{2,1,0:T(8,128)}, u32[]{:S(2)}) copy-start(f32[15,128,512]{2,1,0:T(8,128)} %copy-done.2) | copy-start | bytes 11796484

commit v2 on v1

--- a/solution.py
+++ b/solution.py
@@ -20,7 +20,9 @@
     return lax.dot_general(a, b, (((1,), (1,)), ((), ())), preferred_element_type=F32)
 
 
-def spread_kernel(devices, capacity, f_ref, w_ref, owner_ref, slot_ref, out_ref, tiles_ref):
+def spread_kernel(
+    devices, capacity, visc_ref, f_ref, w_ref, owner_ref, slot_ref, out_ref, splat_ref, tiles_ref
+):
     step = pl.program_id(0)
     group, markers = f_ref.shape
     cells = w_ref.shape[2]
@@ -35,6 +37,8 @@
 
     @pl.when(step == pl.num_programs(0) - 1)
     def _():
+        for x in range(splat_ref.shape[0]):
+            splat_ref[x : x + 1, :] = jnp.full((1, 128), visc_ref[x], F32)
         blocks = owner_ref.shape[1]
         rows = devices * capacity
         owner = owner_ref[...]
@@ -59,26 +63,33 @@
                 out_ref[d, :, cells:] = meta[lo:hi].astype(BF16)
 
 
-def spread(forces, weights, owner, slots, devices, capacity):
+def spread(viscosity, forces, weights, owner, slots, devices, capacity):
     blocks, markers, cells = weights.shape
     group = min(blocks, max(8, 256 // markers))
     return pl.pallas_call(
         functools.partial(spread_kernel, devices, capacity),
-        out_shape=jax.ShapeDtypeStruct((devices, capacity, cells + 128), BF16),
+        out_shape=(
+            jax.ShapeDtypeStruct((devices, capacity, cells + 128), BF16),
+            jax.ShapeDtypeStruct((viscosity.shape[0], 128), F32),
+        ),
         grid=(blocks // group,),
         in_specs=[
+            pl.BlockSpec(memory_space=pltpu.SMEM),
             pl.BlockSpec((group, markers), lambda i: (i, 0)),
             pl.BlockSpec((group, markers, cells), lambda i: (i, 0, 0)),
             pl.BlockSpec((1, blocks), lambda i: (0, 0)),
             pl.BlockSpec((1, blocks), lambda i: (0, 0)),
         ],
-        out_specs=pl.BlockSpec((devices, capacity, cells + 128), lambda i: (0, 0, 0)),
+        out_specs=(
+            pl.BlockSpec((devices, capacity, cells + 128), lambda i: (0, 0, 0)),
+            pl.BlockSpec((viscosity.shape[0], 128), lambda i: (0, 0)),
+        ),
         scratch_shapes=[pltpu.VMEM((blocks, cells), BF16)],
         compiler_params=pltpu.CompilerParams(vmem_limit_bytes=24 << 20),
         cost_estimate=pl.CostEstimate(
             flops=2 * blocks * markers * cells * 64, bytes_accessed=weights.size * 2, transcendentals=0
         ),
-    )(forces, weights, owner, slots)
+    )(viscosity, forces, weights, owner, slots)
 
 
 def factor(visc):
@@ -103,6 +114,26 @@
     for x in range(count - 2, -1, -1):
         right.append(ratio[x] * right[-1])
     return left, right[::-1]
+
+
+def put(ends_ref, which, i, value):
+    rows = ends_ref.shape[2]
+    if rows % 8 == 0:
+        start = pl.multiple_of(lax.rem(i * 8, rows), 8)
+        ends_ref[i * 8 // rows, which, pl.ds(start, 8), :] = value
+    else:
+        share = 8 // rows
+        for k in range(share):
+            ends_ref[i * share + k, which] = value[k * rows : (k + 1) * rows]
+
+
+def get(ends_ref, which, i, lane):
+    rows = ends_ref.shape[2]
+    if rows % 8 == 0:
+        start = pl.multiple_of(lax.rem(i * 8, rows), 8)
+        return ends_ref[i * 8 // rows, which, pl.ds(start, 8), lane]
+    share = 8 // rows
+    return jnp.concatenate([ends_ref[i * share + k, which, :, lane] for k in range(share)], axis=0)
 
 
 def local_kernel(visc_ref, velocity_ref, arrived_ref, out_ref, ends_ref, rhs_ref, coef_ref, flat_ref):
@@ -143,19 +174,19 @@
         for x in range(1, cells_x - 1):
             values.append(side(x) * coef_ref[x] + coef_ref[cells_x + x] * values[-1])
         last = cells_x - 1
-        ends_ref[0, at, :] = side(last) + coef_ref[last] * values[-1]
+        put(ends_ref, 0, i, side(last) + coef_ref[last] * values[-1])
         value = values[-1]
         out_ref[last - 1, at, :] = value
         for x in range(last - 2, -1, -1):
             value = values[x] + coef_ref[cells_x + x] * value
             out_ref[x, at, :] = value
-        ends_ref[1, at, :] = value
+        put(ends_ref, 1, i, value)
         return carry
 
     lax.fori_loop(0, rows_y // 8, chunk, 0, unroll=2)
 
 
-def local_solve(viscosity, velocity, arrived, seg):
+def local_solve(viscosity, velocity, arrived, seg, grid_x):
     cells_x, cells_y, cells_z = velocity.shape
     devices, capacity, width = arrived.shape
     rows = devices * capacity
@@ -163,7 +194,7 @@
         local_kernel,
         out_shape=(
             jax.ShapeDtypeStruct((cells_x - 1, cells_y, cells_z), F32),
-            jax.ShapeDtypeStruct((2, cells_y, cells_z), F32),
+            jax.ShapeDtypeStruct((grid_x, 2, cells_y // grid_x, cells_z), F32),
         ),
         grid=(cells_z // seg,),
         in_specs=[
@@ -173,7 +204,7 @@
         ],
         out_specs=(
             pl.BlockSpec((cells_x - 1, cells_y, seg), lambda i: (0, 0, i)),
-            pl.BlockSpec((2, cells_y, seg), lambda i: (0, 0, i)),
+            pl.BlockSpec((grid_x, 2, cells_y // grid_x, seg), lambda i: (0, 0, 0, i)),
         ),
         scratch_shapes=[
             pltpu.VMEM((cells_y, cells_x * seg), F32),
@@ -184,9 +215,9 @@
     )(viscosity, velocity, arrived)
 
 
-def couple_kernel(visc_ref, out_ref):
-    cells_x, count, lanes = visc_ref.shape
-    visc = [visc_ref[x] for x in range(cells_x)]
+def couple(visc_ref, out_ref):
+    count, cells_x, lanes = visc_ref.shape
+    visc = [visc_ref[:, x, :] for x in range(cells_x)]
     inverse, ratio = factor(visc)
     left, right = spikes(inverse, ratio)
     row = iota((count, lanes), 0)
@@ -210,40 +241,231 @@
     out_ref[3] = jnp.where(row == count - 1, 0.0, sep)
 
 
-def couple(splat):
-    return pl.pallas_call(
-        couple_kernel,
-        out_shape=jax.ShapeDtypeStruct((4,) + splat.shape[1:], F32),
-    )(splat)
-
-
-def reduced_kernel(coef_ref, sides_ref, out_ref):
-    count, rows, cells_z = sides_ref.shape[1:]
+def reduced(coef_ref, sides_ref, out_ref):
+    count, _, rows, cells_z = sides_ref.shape
     lanes = coef_ref.shape[2]
     for c in range(cells_z // lanes):
         at = slice(c * lanes, (c + 1) * lanes)
         values = []
         for d in range(count):
-            side = sides_ref[0, d, :, at]
+            side = sides_ref[d, 0, :, at]
             if d + 1 < count:
-                side = side + coef_ref[3, d : d + 1, :] * sides_ref[1, d + 1, :, at]
+                side = side + coef_ref[3, d : d + 1, :] * sides_ref[d + 1, 1, :, at]
             if d:
                 side = side - coef_ref[2, d : d + 1, :] * values[-1]
             values.append(side * coef_ref[0, d : d + 1, :])
         value = values[-1]
-        out_ref[0, count - 1, :, at] = value
+        out_ref[count - 1, 0, :, at] = value
         for d in range(count - 2, -1, -1):
             value = values[d] - coef_ref[1, d : d + 1, :] * value
-            out_ref[0, d, :, at] = value
-            out_ref[1, d + 1, :, at] = value
-        out_ref[1, 0, :, at] = jnp.zeros_like(value)
-
-
-def reduced(coefs, sides):
+            out_ref[d, 0, :, at] = value
+            out_ref[d + 1, 1, :, at] = value
+        out_ref[0, 1, :, at] = jnp.zeros_like(value)
+
+
+def greet(count, peer_of):
+    barrier = pltpu.get_barrier_semaphore()
+
+    def signal(i, carry):
+        pl.semaphore_signal(
+            barrier, inc=1, device_id=peer_of(i), device_id_type=pl.DeviceIdType.MESH
+        )
+        return carry
+
+    lax.fori_loop(1, count, signal, 0)
+    pl.semaphore_wait(barrier, count - 1)
+
+
+def tiles_kernel(count_x, count_y, out_ref, splat_ref, tiles_ref, whole_ref, send, recv, vsend, vrecv, own):
+    count = count_x * count_y
+    gx, gy = lax.axis_index("gx"), lax.axis_index("gy")
+    me = gx * count_y + gy
+    half = count // 2
+
+    def peer(i):
+        return lax.rem(me + i, count)
+
+    def device(i):
+        return (peer(i) // count_y, lax.rem(peer(i), count_y))
+
+    def line_peer(i):
+        return (lax.rem(gx + i, count_x), gy)
+
+    def tile_copy(i):
+        return pltpu.make_async_remote_copy(
+            src_ref=out_ref.at[peer(i)],
+            dst_ref=tiles_ref.at[me],
+            send_sem=send.at[i],
+            recv_sem=recv.at[i],
+            device_id=device(i),
+            device_id_type=pl.DeviceIdType.MESH,
+        )
+
+    def visc_copy(i):
+        return pltpu.make_async_remote_copy(
+            src_ref=splat_ref,
+            dst_ref=whole_ref.at[gx],
+            send_sem=vsend.at[i],
+            recv_sem=vrecv.at[i],
+            device_id=line_peer(i),
+            device_id_type=pl.DeviceIdType.MESH,
+        )
+
+    own_tile = pltpu.make_async_copy(out_ref.at[me], tiles_ref.at[me], own.at[0])
+    own_visc = pltpu.make_async_copy(splat_ref, whole_ref.at[gx], own.at[1])
+    own_tile.start()
+    own_visc.start()
+    greet(count, device)
+
+    def far(i, carry):
+        tile_copy(half + i).start()
+
+        @pl.when(i > 0)
+        def _():
+            tile_copy(i).start()
+
+        return carry
+
+    lax.fori_loop(0, half, far, 0)
+
+    def start_visc(i, carry):
+        visc_copy(i).start()
+        return carry
+
+    lax.fori_loop(1, count_x, start_visc, 0)
+
+    def finish_tile(i, carry):
+        pltpu.make_async_remote_copy(
+            src_ref=out_ref.at[peer(i)],
+            dst_ref=tiles_ref.at[lax.rem(me + count - i, count)],
+            send_sem=send.at[i],
+            recv_sem=recv.at[i],
+            device_id=device(i),
+            device_id_type=pl.DeviceIdType.MESH,
+        ).wait()
+        return carry
+
+    lax.fori_loop(1, count, finish_tile, 0)
+
+    def finish_visc(i, carry):
+        pltpu.make_async_remote_copy(
+            src_ref=splat_ref,
+            dst_ref=whole_ref.at[lax.rem(gx + count_x - i, count_x)],
+            send_sem=vsend.at[i],
+            recv_sem=vrecv.at[i],
+            device_id=line_peer(i),
+            device_id_type=pl.DeviceIdType.MESH,
+        ).wait()
+        return carry
+
+    lax.fori_loop(1, count_x, finish_visc, 0)
+    own_tile.wait()
+    own_visc.wait()
+
+
+def exchange_tiles(outgoing, splat, count_x, count_y):
+    anywhere = pl.BlockSpec(memory_space=pl.ANY)
+    dma = pltpu.SemaphoreType.DMA
     return pl.pallas_call(
-        reduced_kernel,
-        out_shape=jax.ShapeDtypeStruct(sides.shape, F32),
-    )(coefs, sides)
+        functools.partial(tiles_kernel, count_x, count_y),
+        out_shape=(
+            jax.ShapeDtypeStruct(outgoing.shape, BF16),
+            jax.ShapeDtypeStruct((count_x,) + splat.shape, F32),
+        ),
+        in_specs=[anywhere, anywhere],
+        out_specs=(anywhere, anywhere),
+        scratch_shapes=[
+            dma((count_x * count_y,)),
+            dma((count_x * count_y,)),
+            dma((count_x,)),
+            dma((count_x,)),
+            dma((2,)),
+        ],
+        compiler_params=pltpu.CompilerParams(
+            collective_id=0, has_side_effects=True, vmem_limit_bytes=16 << 20
+        ),
+    )(outgoing, splat)
+
+
+def lines_kernel(
+    count, ends_ref, whole_ref, out_ref, sides_ref, solved_ref, coef_ref, send, recv, back, home, own
+):
+    gx, gy = lax.axis_index("gx"), lax.axis_index("gy")
+
+    def peer(i):
+        return lax.rem(gx + i, count)
+
+    def device(i):
+        return (peer(i), gy)
+
+    def copy(source, target, slot, sends, receives, i):
+        return pltpu.make_async_remote_copy(
+            src_ref=source.at[peer(i)],
+            dst_ref=target.at[slot],
+            send_sem=sends.at[i],
+            recv_sem=receives.at[i],
+            device_id=device(i),
+            device_id_type=pl.DeviceIdType.MESH,
+        )
+
+    def start_all(source, target, sends, receives):
+        half = count // 2
+
+        def start(i, carry):
+            copy(source, target, gx, sends, receives, half + i).start()
+
+            @pl.when(i > 0)
+            def _():
+                copy(source, target, gx, sends, receives, i).start()
+
+            return carry
+
+        lax.fori_loop(0, half, start, 0)
+
+    def finish_all(source, target, sends, receives):
+        def finish(i, carry):
+            copy(source, target, lax.rem(gx + count - i, count), sends, receives, i).wait()
+            return carry
+
+        lax.fori_loop(1, count, finish, 0)
+
+    greet(count, device)
+    start_all(ends_ref, sides_ref, send, recv)
+    mine = pltpu.make_async_copy(ends_ref.at[gx], sides_ref.at[gx], own.at[0])
+    mine.start()
+    couple(whole_ref, coef_ref)
+    mine.wait()
+    finish_all(ends_ref, sides_ref, send, recv)
+    reduced(coef_ref, sides_ref, solved_ref)
+    kept = pltpu.make_async_copy(solved_ref.at[gx], out_ref.at[gx], own.at[1])
+    kept.start()
+    start_all(solved_ref, out_ref, back, home)
+    kept.wait()
+    finish_all(solved_ref, out_ref, back, home)
+
+
+def exchange_lines(ends, whole):
+    count = ends.shape[0]
+    dma = pltpu.SemaphoreType.DMA
+    return pl.pallas_call(
+        functools.partial(lines_kernel, count),
+        out_shape=jax.ShapeDtypeStruct(ends.shape, F32),
+        in_specs=[pl.BlockSpec(memory_space=pltpu.VMEM)] * 2,
+        out_specs=pl.BlockSpec(memory_space=pltpu.VMEM),
+        scratch_shapes=[
+            pltpu.VMEM(ends.shape, F32),
+            pltpu.VMEM(ends.shape, F32),
+            pltpu.VMEM((4, count, 128), F32),
+            dma((count,)),
+            dma((count,)),
+            dma((count,)),
+            dma((count,)),
+            dma((2,)),
+        ],
+        compiler_params=pltpu.CompilerParams(
+            collective_id=1, has_side_effects=True, vmem_limit_bytes=16 << 20
+        ),
+    )(ends, whole)
 
 
 def final_kernel(visc_ref, inner_ref, ends_ref, out_ref, coef_ref):
@@ -262,7 +484,7 @@
         at = pl.ds(pl.multiple_of(i * 8, 8), 8)
         for c in range(cells_z // seg):
             lane = slice(c * seg, (c + 1) * seg)
-            own, before = ends_ref[0, at, lane], ends_ref[1, at, lane]
+            own, before = get(ends_ref, 0, i, lane), get(ends_ref, 1, i, lane)
             for x in range(count):
                 out_ref[x, at, lane] = (
                     inner_ref[x, at, lane] + coef_ref[x] * before + coef_ref[count + x] * own
@@ -284,7 +506,7 @@
         in_specs=[
             pl.BlockSpec(memory_space=pltpu.SMEM),
             pl.BlockSpec((count, rows, cells_z), lambda i: (0, i, 0)),
-            pl.BlockSpec((2, rows, cells_z), lambda i: (0, i, 0)),
+            pl.BlockSpec((ends.shape[0] // parts,) + ends.shape[1:], lambda i: (i, 0, 0, 0)),
         ],
         out_specs=pl.BlockSpec((count + 1, rows, cells_z), lambda i: (0, i, 0)),
         scratch_shapes=[pltpu.VMEM((2 * count, 8, seg), F32)],
@@ -299,9 +521,8 @@
     blocks, _, cells = spread_weights.shape
     capacity = max(2, 2 * blocks // devices)
     seg = cells // cells_x
-    whole = lax.all_gather(viscosity, "gx", axis=0, tiled=True).reshape(grid_x, cells_x)
-    splat = jnp.broadcast_to(whole.T[:, :, None], (cells_x, grid_x, 128))
-    outgoing = spread(
+    outgoing, splat = spread(
+        viscosity,
         marker_forces,
         spread_weights,
         block_owner.reshape(1, blocks),
@@ -309,14 +530,10 @@
         devices,
         capacity,
     )
-    arrived = lax.all_to_all(outgoing, ("gx", "gy"), split_axis=0, concat_axis=0, tiled=True)
-    coefs = couple(splat)
-    inner, ends = local_solve(viscosity, velocity, arrived, seg)
-    sides = lax.all_to_all(
-        ends.reshape(2, grid_x, -1, cells_z), "gx", split_axis=1, concat_axis=1, tiled=True
-    )
-    returned = lax.all_to_all(reduced(coefs, sides), "gx", split_axis=1, concat_axis=1, tiled=True)
-    return final(viscosity, inner, returned.reshape(2, cells_y, cells_z), seg)
+    arrived, whole = exchange_tiles(outgoing, splat, grid_x, devices // grid_x)
+    inner, ends = local_solve(viscosity, velocity, arrived, seg, grid_x)
+    returned = exchange_lines(ends, whole)
+    return final(viscosity, inner, returned, seg)
 
 
 def solution(mesh):

time: 124 us -> 86.1 us (0.69)
  blocking collectives: 88.3 us -> 0 us
  Pallas kernels: 16.6 us -> 79.7 us
  local copies, waits for them, and re-layouts: 14.1 us -> 6.15 us
  starting transfers between devices: 3.57 us -> 0 us
    pallas_call x2, Pallas kernels: 3.84 us -> 66.4 us  [the longest x1 35.7 us: exchange_tiles(): pl.pallas_call(functools.partial(tiles_kernel, count_x, count_y), out_sha...]
    all_to_all x2 -> x0, blocking collectives: 53.1 us -> none  [the longest x1 36.2 us: per_device(): lax.all_to_all(outgoing, ('gx', 'gy'), split_axis=0, concat_axis=0, tiled...]
    unnamed x1 -> x0, blocking collectives: 35.1 us -> none
    unnamed x20 -> x11, local copies, waits for them, and re-layouts: 10.4 us -> 6.15 us
    all_to_all x1 -> x0, starting transfers between devices: 3.57 us -> none  [per_device(): lax.all_to_all(ends.reshape(2, grid_x, -1, cells_z), 'gx', split_axis=1,...]
  transfers between devices with their start and end apart: 1 -> 0, of which waited for: 0 -> 0; matrix products, arithmetic and copies ran while one was open for 1% -> 0% of each run, Pallas kernels for 1% -> 0%
where the time goes in v2:
time: 86.1 us; the launch traced here: 85.9 us
  Pallas kernels  79.7 us (93%)
  local copies, waits for them, and re-layouts  6.15 us (7%)
    pallas_call x1, Pallas kernels, exchange_tiles(): pl.pallas_call(functools.partial(tiles_kernel, count_x, count_y), out_sha...  35.7 us
    pallas_call x1, Pallas kernels, exchange_lines(): pl.pallas_call(functools.partial(lines_kernel, count), out_shape=jax.Shap...  30.6 us
    unnamed x11, local copies, waits for them, and re-layouts  6.15 us
    pallas_call x1, Pallas kernels, local_solve(): pl.pallas_call(local_kernel, out_shape=(jax.ShapeDtypeStruct((cells_x - 1...  5.93 us
    pallas_call x1, Pallas kernels, spread(): pl.pallas_call(functools.partial(spread_kernel, devices, capacity), out_s...  3.86 us
    pallas_call x1, Pallas kernels, final(): pl.pallas_call(final_kernel, out_shape=jax.ShapeDtypeStruct((count + 1, c...  3.54 us

profile of v2, /device:TPU:0, one launch (start us, length us, event | category | flops | bytes accessed | tf_op | source)
XLA Modules:
  0.0 85.9 jit_solution(11505123997024834064)
XLA Ops:
  0.0 0.8 copy.7.f_ref
  0.8 0.0 copy-start
  0.8 3.4 %copy-done = bf16[128,16,2048]{2,1,0:T(8,128)(2,1)S(1)} copy-done((bf16[128,16,2048]{2,1,0:T(8,128)(2,1)S(1)}, bf16[128,16,2048]{2,1,0:T(8,128)(2,1)}, u32[]{:S(2)}) %copy-start) | copy-done | bytes 8388632
  4.2 0.0 copy-start.2
  4.2 0.7 copy-done.2
  4.8 0.0 copy-start.3
  4.8 0.7 copy-done.3
  5.5 0.0 copy-start.4
  5.5 0.7 copy-done.4
  6.2 0.0 copy-start.1
  6.2 3.9 %shard_map.64 = (bf16[32,8,2176]{2,1,0:T(8,128)(2,1)S(1)}, f32[16,128]{1,0:T(8,128)S(1)}) custom-call(f32[16]{0:T(128)S(1)} %copy-done.2, bf16[128,16]{1,0:T(8,128)(2,1)S(1)} %copy.7.f_ref, bf16[128,16,2048]{2,1,0:T(8,128)(2,1)S(1)} %copy-done, s32[1,128]{1,0:T(1,128)S(1)} %bitcast.2, s32[1,128]{1,0:T(1,128)S(1)} %bitcast.3), custom_call_target="tpu_custom_call" | custom-call | flops 536870912 | bytes 8388608 | tf_op jit(solution)/shard_map/pallas_call | solution.py:69
  10.0 35.7 %shard_map.65 = (bf16[32,8,2176]{2,1,0:T(8,128)(2,1)S(1)}, f32[16,16,128]{2,1,0:T(8,128)S(1)}) custom-call(bf16[32,8,2176]{2,1,0:T(8,128)(2,1)S(1)} %get-tuple-element.11.out_ref, f32[16,128]{1,0:T(8,128)S(1)} %get-tuple-element.12.splat_ref), custom_call_target="tpu_custom_call" | custom-call | tf_op jit(solution)/shard_map/pallas_call | solution.py:369
  45.7 0.0 copy-done.1
  45.8 5.9 %shard_map.66 = (f32[15,128,512]{2,1,0:T(8,128)S(1)}, f32[16,2,8,512]{3,2,1,0:T(8,128)S(1)}) custom-call(f32[16]{0:T(128)S(1)} %copy-done.2, f32[16,128,512]{2,1,0:T(8,128)S(1)} %copy-done.1, bf16[32,8,2176]{2,1,0:T(8,128)(2,1)S(1)} %get-tuple-element.13.arrived_ref), custom_call_target="tpu_custom_call" | custom-call | tf_op jit(solution)/shard_map/pallas_call | solution.py:193
  51.7 30.6 %shard_map.67.ends_ref = f32[16,2,8,512]{3,2,1,0:T(8,128)S(1)} custom-call(f32[16,2,8,512]{3,2,1,0:T(8,128)S(1)} %get-tuple-element.15.ends_ref, f32[16,16,128]{2,1,0:T(8,128)S(1)} %get-tuple-element.16.whole_ref), custom_call_target="tpu_custom_call" | custom-call | tf_op jit(solution)/shard_map/pallas_call | solution.py:450
  82.4 3.5 %shard_map.68 = f32[16,128,512]{2,1,0:T(8,128)} custom-call(f32[16]{0:T(128)S(1)} %copy-done.2, f32[15,128,512]{2,1,0:T(8,128)S(1)} %get-tuple-element.14.inner_ref, f32[16,2,8,512]{3,2,1,0:T(8,128)S(1)} %shard_map.67.ends_ref), custom_call_target="tpu_custom_call" | custom-call | tf_op jit(solution)/shard_map/pallas_call | solution.py:502
Async XLA Ops:
  0.8 3.4 %copy-start = (bf16[128,16,2048]{2,1,0:T(8,128)(2,1)S(1)}, bf16[128,16,2048]{2,1,0:T(8,128)(2,1)}, u32[]{:S(2)}) copy-start(bf16[128,16,2048]{2,1,0:T(8,128)(2,1)} %w_ref.1) | copy-start | bytes 25165828
  4.2 0.7 copy-start.2
  4.8 0.7 copy-start.3
  5.5 0.7 copy-start.4
  6.2 39.6 %copy-start.1 = (f32[16,128,512]{2,1,0:T(8,128)S(1)}, f32[16,128,512]{2,1,0:T(8,128)}, u32[]{:S(2)}) copy-start(f32[16,128,512]{2,1,0:T(8,128)} %velocity_ref.1) | copy-start | bytes 12582916

commit v3 on v2

--- a/solution.py
+++ b/solution.py
@@ -127,13 +127,14 @@
             ends_ref[i * share + k, which] = value[k * rows : (k + 1) * rows]
 
 
-def get(ends_ref, which, i, lane):
-    rows = ends_ref.shape[2]
+def get(ref, i, lane):
+    rows = ref.shape[1]
     if rows % 8 == 0:
         start = pl.multiple_of(lax.rem(i * 8, rows), 8)
-        return ends_ref[i * 8 // rows, which, pl.ds(start, 8), lane]
+        return ref[i * 8 // rows, pl.ds(start, 8), lane].astype(F32)
     share = 8 // rows
-    return jnp.concatenate([ends_ref[i * share + k, which, :, lane] for k in range(share)], axis=0)
+    parts = [ref[i * share + k, :, lane].astype(F32) for k in range(share)]
+    return jnp.concatenate(parts, axis=0)
 
 
 def local_kernel(visc_ref, velocity_ref, arrived_ref, out_ref, ends_ref, rhs_ref, coef_ref, flat_ref):
@@ -241,7 +242,7 @@
     out_ref[3] = jnp.where(row == count - 1, 0.0, sep)
 
 
-def reduced(coef_ref, sides_ref, out_ref):
+def reduced(coef_ref, sides_ref, out_ref, step_ref):
     count, _, rows, cells_z = sides_ref.shape
     lanes = coef_ref.shape[2]
     for c in range(cells_z // lanes):
@@ -255,12 +256,23 @@
                 side = side - coef_ref[2, d : d + 1, :] * values[-1]
             values.append(side * coef_ref[0, d : d + 1, :])
         value = values[-1]
-        out_ref[count - 1, 0, :, at] = value
+        out_ref[count - 1, :, at] = value
         for d in range(count - 2, -1, -1):
-            value = values[d] - coef_ref[1, d : d + 1, :] * value
-            out_ref[d, 0, :, at] = value
-            out_ref[d + 1, 1, :, at] = value
-        out_ref[0, 1, :, at] = jnp.zeros_like(value)
+            before = values[d] - coef_ref[1, d : d + 1, :] * value
+            out_ref[d, :, at] = before
+            step_ref[d + 1, :, at] = (before - value).astype(BF16)
+            value = before
+        step_ref[0, :, at] = (-value).astype(BF16)
+
+
+def partner(me, k, count, sign=1):
+    if count & (count - 1):
+        return lax.rem(me + count + sign * k, count)
+    total, bit = 0, 1
+    while bit < count:
+        total = total + bit * lax.rem(lax.rem(me // bit, 2) + lax.rem(k // bit, 2), 2)
+        bit *= 2
+    return total
 
 
 def greet(count, peer_of):
@@ -280,34 +292,29 @@
     count = count_x * count_y
     gx, gy = lax.axis_index("gx"), lax.axis_index("gy")
     me = gx * count_y + gy
-    half = count // 2
-
-    def peer(i):
-        return lax.rem(me + i, count)
 
     def device(i):
-        return (peer(i) // count_y, lax.rem(peer(i), count_y))
-
-    def line_peer(i):
-        return (lax.rem(gx + i, count_x), gy)
-
-    def tile_copy(i):
+        peer = partner(me, i, count)
+        return (peer // count_y, lax.rem(peer, count_y))
+
+    def tile_copy(i, slot):
+        peer = partner(me, i, count)
         return pltpu.make_async_remote_copy(
-            src_ref=out_ref.at[peer(i)],
-            dst_ref=tiles_ref.at[me],
+            src_ref=out_ref.at[peer],
+            dst_ref=tiles_ref.at[slot],
             send_sem=send.at[i],
             recv_sem=recv.at[i],
-            device_id=device(i),
+            device_id=(peer // count_y, lax.rem(peer, count_y)),
             device_id_type=pl.DeviceIdType.MESH,
         )
 
-    def visc_copy(i):
+    def visc_copy(i, slot):
         return pltpu.make_async_remote_copy(
             src_ref=splat_ref,
-            dst_ref=whole_ref.at[gx],
+            dst_ref=whole_ref.at[slot],
             send_sem=vsend.at[i],
             recv_sem=vrecv.at[i],
-            device_id=line_peer(i),
+            device_id=(partner(gx, i, count_x), gy),
             device_id_type=pl.DeviceIdType.MESH,
         )
 
@@ -317,47 +324,25 @@
     own_visc.start()
     greet(count, device)
 
-    def far(i, carry):
-        tile_copy(half + i).start()
-
-        @pl.when(i > 0)
-        def _():
-            tile_copy(i).start()
-
-        return carry
-
-    lax.fori_loop(0, half, far, 0)
+    def start_tile(i, carry):
+        tile_copy(i, me).start()
+        return carry
 
     def start_visc(i, carry):
-        visc_copy(i).start()
-        return carry
-
+        visc_copy(i, gx).start()
+        return carry
+
+    def finish_tile(i, carry):
+        tile_copy(i, partner(me, i, count, -1)).wait()
+        return carry
+
+    def finish_visc(i, carry):
+        visc_copy(i, partner(gx, i, count_x, -1)).wait()
+        return carry
+
+    lax.fori_loop(1, count, start_tile, 0)
     lax.fori_loop(1, count_x, start_visc, 0)
-
-    def finish_tile(i, carry):
-        pltpu.make_async_remote_copy(
-            src_ref=out_ref.at[peer(i)],
-            dst_ref=tiles_ref.at[lax.rem(me + count - i, count)],
-            send_sem=send.at[i],
-            recv_sem=recv.at[i],
-            device_id=device(i),
-            device_id_type=pl.DeviceIdType.MESH,
-        ).wait()
-        return carry
-
     lax.fori_loop(1, count, finish_tile, 0)
-
-    def finish_visc(i, carry):
-        pltpu.make_async_remote_copy(
-            src_ref=splat_ref,
-            dst_ref=whole_ref.at[lax.rem(gx + count_x - i, count_x)],
-            send_sem=vsend.at[i],
-            recv_sem=vrecv.at[i],
-            device_id=line_peer(i),
-            device_id_type=pl.DeviceIdType.MESH,
-        ).wait()
-        return carry
-
     lax.fori_loop(1, count_x, finish_visc, 0)
     own_tile.wait()
     own_visc.wait()
@@ -388,79 +373,85 @@
 
 
 def lines_kernel(
-    count, ends_ref, whole_ref, out_ref, sides_ref, solved_ref, coef_ref, send, recv, back, home, own
+    count, ends_ref, whole_ref, out_ref, step_ref,
+    sides_ref, solved_ref, steps_ref, coef_ref, send, recv, back, home, back_step, home_step, own
 ):
     gx, gy = lax.axis_index("gx"), lax.axis_index("gy")
 
-    def peer(i):
-        return lax.rem(gx + i, count)
-
     def device(i):
-        return (peer(i), gy)
+        return (partner(gx, i, count), gy)
 
     def copy(source, target, slot, sends, receives, i):
+        peer = partner(gx, i, count)
         return pltpu.make_async_remote_copy(
-            src_ref=source.at[peer(i)],
+            src_ref=source.at[peer],
             dst_ref=target.at[slot],
             send_sem=sends.at[i],
             recv_sem=receives.at[i],
-            device_id=device(i),
+            device_id=(peer, gy),
             device_id_type=pl.DeviceIdType.MESH,
         )
 
-    def start_all(source, target, sends, receives):
-        half = count // 2
-
+    def start_all(*groups):
         def start(i, carry):
-            copy(source, target, gx, sends, receives, half + i).start()
-
-            @pl.when(i > 0)
-            def _():
+            for source, target, sends, receives in groups:
                 copy(source, target, gx, sends, receives, i).start()
-
             return carry
 
-        lax.fori_loop(0, half, start, 0)
-
-    def finish_all(source, target, sends, receives):
+        lax.fori_loop(1, count, start, 0)
+
+    def finish_all(*groups):
         def finish(i, carry):
-            copy(source, target, lax.rem(gx + count - i, count), sends, receives, i).wait()
+            for source, target, sends, receives in groups:
+                copy(source, target, partner(gx, i, count, -1), sends, receives, i).wait()
             return carry
 
         lax.fori_loop(1, count, finish, 0)
 
+    outward = (ends_ref, sides_ref, send, recv)
+    homeward = (
+        (solved_ref, out_ref, back, home),
+        (steps_ref, step_ref, back_step, home_step),
+    )
     greet(count, device)
-    start_all(ends_ref, sides_ref, send, recv)
+    start_all(outward)
     mine = pltpu.make_async_copy(ends_ref.at[gx], sides_ref.at[gx], own.at[0])
     mine.start()
     couple(whole_ref, coef_ref)
     mine.wait()
-    finish_all(ends_ref, sides_ref, send, recv)
-    reduced(coef_ref, sides_ref, solved_ref)
+    finish_all(outward)
+    reduced(coef_ref, sides_ref, solved_ref, steps_ref)
     kept = pltpu.make_async_copy(solved_ref.at[gx], out_ref.at[gx], own.at[1])
+    kept_step = pltpu.make_async_copy(steps_ref.at[gx], step_ref.at[gx], own.at[2])
     kept.start()
-    start_all(solved_ref, out_ref, back, home)
+    kept_step.start()
+    start_all(*homeward)
     kept.wait()
-    finish_all(solved_ref, out_ref, back, home)
+    kept_step.wait()
+    finish_all(*homeward)
 
 
 def exchange_lines(ends, whole):
     count = ends.shape[0]
+    single = (count,) + ends.shape[2:]
     dma = pltpu.SemaphoreType.DMA
     return pl.pallas_call(
         functools.partial(lines_kernel, count),
-        out_shape=jax.ShapeDtypeStruct(ends.shape, F32),
+        out_shape=(jax.ShapeDtypeStruct(single, F32), jax.ShapeDtypeStruct(single, BF16)),
         in_specs=[pl.BlockSpec(memory_space=pltpu.VMEM)] * 2,
-        out_specs=pl.BlockSpec(memory_space=pltpu.VMEM),
+        out_specs=(pl.BlockSpec(memory_space=pltpu.VMEM),) * 2,
         scratch_shapes=[
             pltpu.VMEM(ends.shape, F32),
-            pltpu.VMEM(ends.shape, F32),
+            pltpu.VMEM(single, F32),
+            pltpu.VMEM(single, BF16),
             pltpu.VMEM((4, count, 128), F32),
             dma((count,)),
             dma((count,)),
             dma((count,)),
             dma((count,)),
-            dma((2,)),
+            dma((count,)),
+            dma((count,)),
+            dma((3,)),
         ],
         compiler_params=pltpu.CompilerParams(
             collective_id=1, has_side_effects=True, vmem_limit_bytes=16 << 20
@@ -468,7 +459,7 @@
     )(ends, whole)
 
 
-def final_kernel(visc_ref, inner_ref, ends_ref, out_ref, coef_ref):
+def final_kernel(visc_ref, inner_ref, own_ref, step_ref, out_ref, coef_ref):
     count, rows_y, cells_z = inner_ref.shape
     seg = coef_ref.shape[2]
 
@@ -484,7 +475,8 @@
         at = pl.ds(pl.multiple_of(i * 8, 8), 8)
         for c in range(cells_z // seg):
             lane = slice(c * seg, (c + 1) * seg)
-            own, before = get(ends_ref, 0, i, lane), get(ends_ref, 1, i, lane)
+            own = get(own_ref, i, lane)
+            before = own + get(step_ref, i, lane)
             for x in range(count):
                 out_ref[x, at, lane] = (
                     inner_ref[x, at, lane] + coef_ref[x] * before + coef_ref[count + x] * own
@@ -495,7 +487,7 @@
     lax.fori_loop(0, rows_y // 8, chunk, 0)
 
 
-def final(viscosity, inner, ends, seg):
+def final(viscosity, inner, own, step, seg):
     count, cells_y, cells_z = inner.shape
     parts = 4
     rows = cells_y // parts
@@ -506,12 +498,13 @@
         in_specs=[
             pl.BlockSpec(memory_space=pltpu.SMEM),
             pl.BlockSpec((count, rows, cells_z), lambda i: (0, i, 0)),
-            pl.BlockSpec((ends.shape[0] // parts,) + ends.shape[1:], lambda i: (i, 0, 0, 0)),
+            pl.BlockSpec((own.shape[0] // parts,) + own.shape[1:], lambda i: (i, 0, 0)),
+            pl.BlockSpec((own.shape[0] // parts,) + own.shape[1:], lambda i: (i, 0, 0)),
         ],
         out_specs=pl.BlockSpec((count + 1, rows, cells_z), lambda i: (0, i, 0)),
         scratch_shapes=[pltpu.VMEM((2 * count, 8, seg), F32)],
         compiler_params=pltpu.CompilerParams(vmem_limit_bytes=24 << 20),
-    )(viscosity, inner, ends)
+    )(viscosity, inner, own, step)
 
 
 def per_device(velocity, viscosity, marker_forces, spread_weights, block_owner, tile_slot):
@@ -524,7 +517,7 @@
     outgoing, splat = spread(
         viscosity,
         marker_forces,
-        spread_weights,
+        pltpu.with_memory_space_constraint(spread_weights, pltpu.HBM),
         block_owner.reshape(1, blocks),
         tile_slot.reshape(1, blocks),
         devices,
@@ -532,8 +525,8 @@
     )
     arrived, whole = exchange_tiles(outgoing, splat, grid_x, devices // grid_x)
     inner, ends = local_solve(viscosity, velocity, arrived, seg, grid_x)
-    returned = exchange_lines(ends, whole)
-    return final(viscosity, inner, returned, seg)
+    own, step = exchange_lines(ends, whole)
+    return final(viscosity, inner, own, step, seg)
 
 
 def solution(mesh):

time: 86.1 us -> 85 us (0.987)
  local copies, waits for them, and re-layouts: 6.15 us -> 2.77 us
  Pallas kernels: 79.7 us -> 81.9 us
    pallas_call x1, Pallas kernels: 3.86 us -> 7.67 us  [spread(): pl.pallas_call(functools.partial(spread_kernel, devices, capacity), out_s...]
    unnamed x11 -> x9, local copies, waits for them, and re-layouts: 6.15 us -> 2.77 us
    pallas_call x1, Pallas kernels: 30.6 us -> 28 us  [exchange_lines(): pl.pallas_call(functools.partial(lines_kernel, count), out_shape=(jax.Sha...]
    pallas_call x1, Pallas kernels: 35.7 us -> 36.8 us  [exchange_tiles(): pl.pallas_call(functools.partial(tiles_kernel, count_x, count_y), out_sha...]
where the time goes in v3:
time: 85 us; the launch traced here: 84.8 us
  Pallas kernels  81.9 us (96%)
  local copies, waits for them, and re-layouts  2.77 us (3%)
    pallas_call x1, Pallas kernels, exchange_tiles(): pl.pallas_call(functools.partial(tiles_kernel, count_x, count_y), out_sha...  36.8 us
    pallas_call x1, Pallas kernels, exchange_lines(): pl.pallas_call(functools.partial(lines_kernel, count), out_shape=(jax.Sha...  28 us
    pallas_call x1, Pallas kernels, spread(): pl.pallas_call(functools.partial(spread_kernel, devices, capacity), out_s...  7.67 us
    pallas_call x1, Pallas kernels, local_solve(): pl.pallas_call(local_kernel, out_shape=(jax.ShapeDtypeStruct((cells_x - 1...  5.93 us
    pallas_call x1, Pallas kernels, final(): pl.pallas_call(final_kernel, out_shape=jax.ShapeDtypeStruct((count + 1, c...  3.59 us
    unnamed x9, local copies, waits for them, and re-layouts  2.77 us

profile of v3, /device:TPU:0, one launch (start us, length us, event | category | flops | bytes accessed | tf_op | source)
XLA Modules:
  0.0 84.8 jit_solution(9249506222475462993)
XLA Ops:
  0.0 0.8 copy.7.f_ref
  0.8 0.0 copy-start.1
  0.8 0.7 copy-done.1
  1.5 0.0 copy-start.2
  1.5 0.7 copy-done.2
  2.1 0.0 copy-start.3
  2.1 0.7 copy-done.3
  2.8 0.0 copy-start
  2.8 7.7 %shard_map.64 = (bf16[32,8,2176]{2,1,0:T(8,128)(2,1)S(1)}, f32[16,128]{1,0:T(8,128)S(1)}) custom-call(f32[16]{0:T(128)S(1)} %copy-done.1, bf16[128,16]{1,0:T(8,128)(2,1)S(1)} %copy.7.f_ref, bf16[128,16,2048]{2,1,0:T(8,128)(2,1)} %w_ref.1, s32[1,128]{1,0:T(1,128)S(1)} %bitcast.2, s32[1,128]{1,0:T(1,128)S(1)} %bitcast.3), custom_call_target="tpu_custom_call" | custom-call | flops 536870912 | bytes 8388608 | tf_op jit(solution)/shard_map/pallas_call | solution.py:69
  10.5 36.8 %shard_map.65 = (bf16[32,8,2176]{2,1,0:T(8,128)(2,1)S(1)}, f32[16,16,128]{2,1,0:T(8,128)S(1)}) custom-call(bf16[32,8,2176]{2,1,0:T(8,128)(2,1)S(1)} %get-tuple-element.13.out_ref, f32[16,128]{1,0:T(8,128)S(1)} %get-tuple-element.14.splat_ref), custom_call_target="tpu_custom_call" | custom-call | tf_op jit(solution)/shard_map/pallas_call | solution.py:354
  47.3 0.0 copy-done
  47.3 5.9 %shard_map.66 = (f32[15,128,512]{2,1,0:T(8,128)S(1)}, f32[16,2,8,512]{3,2,1,0:T(8,128)S(1)}) custom-call(f32[16]{0:T(128)S(1)} %copy-done.1, f32[16,128,512]{2,1,0:T(8,128)S(1)} %copy-done, bf16[32,8,2176]{2,1,0:T(8,128)(2,1)S(1)} %get-tuple-element.15.arrived_ref), custom_call_target="tpu_custom_call" | custom-call | tf_op jit(solution)/shard_map/pallas_call | solution.py:194
  53.2 28.0 %shard_map.67 = (f32[16,8,512]{2,1,0:T(8,128)S(1)}, bf16[16,8,512]{2,1,0:T(8,128)(2,1)S(1)}) custom-call(f32[16,2,8,512]{3,2,1,0:T(8,128)S(1)} %get-tuple-element.17.ends_ref, f32[16,16,128]{2,1,0:T(8,128)S(1)} %get-tuple-element.18.whole_ref), custom_call_target="tpu_custom_call" | custom-call | tf_op jit(solution)/shard_map/pallas_call | solution.py:438
  81.2 3.6 %shard_map.68 = f32[16,128,512]{2,1,0:T(8,128)} custom-call(f32[16]{0:T(128)S(1)} %copy-done.1, f32[15,128,512]{2,1,0:T(8,128)S(1)} %get-tuple-element.16.inner_ref, f32[16,8,512]{2,1,0:T(8,128)S(1)} %get-tuple-element.19.own_ref, bf16[16,8,512]{2,1,0:T(8,128)(2,1)S(1)} %get-tuple-element.20.step_ref), custom_call_target="tpu_custom_call" | custom-call | tf_op jit(solution)/shard_map/pallas_call | solution.py:494
Async XLA Ops:
  0.8 0.7 copy-start.1
  1.5 0.7 copy-start.2
  2.1 0.7 copy-start.3
  2.8 44.5 %copy-start = (f32[16,128,512]{2,1,0:T(8,128)S(1)}, f32[16,128,512]{2,1,0:T(8,128)}, u32[]{:S(2)}) copy-start(f32[16,128,512]{2,1,0:T(8,128)} %velocity_ref.1) | copy-start | bytes 12582916
